TPU v7x, 32 devices: a whole 2x2x4 slice. The times are simulated.
32 devices in a mesh: tm: 2 (over x), chan: 4 (over y, core), bl: 4 (over z).
Axes of the slice: x: 2, y: 2, z: 4, core: 2. Of those that a mesh axis runs over, the one named last changes fastest.
Arguments:
- voltages: bfloat16 [2, 256, 128, 512], P(None, ('chan', 'bl'), None, 'tm'), may hold values from -6 to 6
Outputs:
- visibilities: bfloat16 [2, 128, 4, 256, 256], P(None, ('chan', 'bl'), 'tm')
All inputs are finite; a program needn't handle non-finite values.
Results may differ from a plain program's by a relative error of at most 0.0051.
Values may be sent and summed in bfloat16 or wider, within the bound.
A program may use at most 64 MiB of HBM per device.

v0:
```python
import jax
import jax.numpy as jnp
from jax import lax
from jax.sharding import PartitionSpec as P

HALF = 128


def passed_along(block, axis, distance):
    devices = range(lax.axis_size(axis))
    route = [(i - distance, i) for i in devices if i - distance in devices]
    return lax.ppermute(block, axis, route)


def tapers(length):
    steps = jnp.arange(length, dtype=jnp.float32)
    taper_early = jnp.sin(jnp.pi * (steps + 0.5) / (2.0 * length))
    taper_late = jnp.sin(jnp.pi * (steps + 0.5 + length) / (2.0 * length))
    return (taper_early, taper_late)


def weighted(block, taper):
    return (block.astype(jnp.float32) * taper).astype(jnp.bfloat16)


def products(stacked):
    signals = stacked.shape[0] // 2
    gram = jnp.einsum("pct,qct->cpq", stacked, stacked, preferred_element_type=jnp.float32)
    real_part = gram[:, :signals, :signals] + gram[:, signals:, signals:]
    imag_part = gram[:, signals:, :signals] - gram[:, :signals, signals:]
    return (real_part, imag_part)


def local(voltages):
    turned = lax.all_to_all(voltages, ("chan", "bl"), split_axis=2, concat_axis=1, tiled=True)
    signals = turned.shape[1]
    channels = turned.shape[2]
    samples = turned.shape[3]
    halves = samples // HALF
    scale = 1.0 / HALF
    taper_early, taper_late = tapers(HALF)
    stacked = turned.reshape(2 * signals, channels, samples)
    lates = []
    earlies = []
    for index in range(halves):
        piece = stacked[:, :, index * HALF : (index + 1) * HALF]
        lates.append(products(weighted(piece, taper_late)))
        if index + 1 < halves:
            earlies.append(products(weighted(piece, taper_early)))
    tail = turned[:, :, :, samples - HALF :]
    received = passed_along(tail, "tm", 1)
    previous = products(weighted(received.reshape(2 * signals, channels, HALF), taper_early))
    real_list = []
    imag_list = []
    for index in range(halves):
        late_real, late_imag = lates[index]
        real_list.append(((late_real + previous[0]) * scale).astype(jnp.bfloat16))
        imag_list.append(((late_imag + previous[1]) * scale).astype(jnp.bfloat16))
        if index + 1 < halves:
            previous = earlies[index]
    return jnp.stack([jnp.stack(real_list, 1), jnp.stack(imag_list, 1)], 0)


def solution(mesh):
    return jax.shard_map(
        local,
        mesh=mesh,
        in_specs=(P(None, ("chan", "bl"), None, "tm"),),
        out_specs=P(None, ("chan", "bl"), "tm", None, None),
        check_vma=False,
    )
```

profile of v0, /device:TPU:0, one launch (start us, length us, event | category | flops | bytes accessed | tf_op | source)
XLA Modules:
  0.0 100.2 jit_solution(14008793336782749242)
XLA Ops:
  0.0 2.8 %copy.22 = bf16[2,16,128,256]{3,1,0,2:T(8,128)(2,1)S(1)} copy(bf16[2,16,128,256]{3,2,1,0:T(8,128)(2,1)} %param.1) | data formatting | bytes 4194304 | tf_op args[0]
  2.8 56.5 %all_to_all.18 = bf16[2,16,128,256]{3,1,0,2:T(8,128)(2,1)S(1)} all-to-all(bf16[2,16,128,256]{3,1,0,2:T(8,128)(2,1)S(1)} %copy.22), channel_id=1, replica_groups=mesh['tm'=2,'chan'=4,'bl'=4] {'chan','bl'}, dimensions={2} | all-to-all | bytes 4194304 | tf_op jit(solution)/shard_map/all_to_all | solution.py:35
  59.3 1.7 %copy.24 = bf16[2,16,16,8,256]{4,3,2,1,0:T(8,128)(2,1)S(1)} copy(bf16[2,16,16,8,256]{4,2,0,3,1:T(8,128)(2,1)S(1)} %bitcast.24) | data formatting | bytes 4194304 | tf_op jit(solution)/shard_map/all_to_all | solution.py:35
  61.0 0.1 slice.79
  61.1 3.6 %collective-permute-start = (bf16[2,256,8,128]{3,2,1,0:T(8,128)(2,1)S(1)}, bf16[2,256,8,128]{3,2,1,0:T(8,128)(2,1)S(1)}, u32[]{:S(2)}, u32[]{:S(2)}) collective-permute-start(bf16[2,256,8,128]{3,2,1,0:T(8,128)(2,1)S(1)} %slice.79), channel_id=1, source_target_pairs={{0,16},{1,17},{2,18},{3,19},{4,20},{5,21},{6,22},{7,23},{8,24},{9,... | collective-permute-start | bytes 3145736 | tf_op jit(solution)/shard_map/ppermute | solution.py:12
  64.7 0.1 multiply_sine_fusion
  64.8 22.0 %collective-permute-done = bf16[2,256,8,128]{3,2,1,0:T(8,128)(2,1)S(1)} collective-permute-done((bf16[2,256,8,128]{3,2,1,0:T(8,128)(2,1)S(1)}, bf16[2,256,8,128]{3,2,1,0:T(8,128)(2,1)S(1)}, u32[]{:S(2)}, u32[]{:S(2)}) %collective-permute-start) | collective-permute-done | bytes 1048608 | tf_op jit(solution)/shard_map/ppermute | solution.py:12
  86.8 0.8 fusion
  87.7 1.3 %fusion.23 = f32[8,512,512]{2,1,0:T(8,128)S(1)} fusion(bf16[512,8,128]{2,1,0:T(8,128)(2,1)S(1)} %get-tuple-element.12), kind=kOutput, calls=%fused_computation.38 | convolution fusion | flops 536870912 | bytes 9437184 | tf_op jit(solution)/shard_map/pct,qct->cpq/dot_general | solution.py:28
  88.9 1.3 %fusion.25 = f32[8,512,512]{2,1,0:T(8,128)S(1)} fusion(bf16[512,8,128]{2,1,0:T(8,128)(2,1)S(1)} %get-tuple-element.9), kind=kOutput, calls=%fused_computation.40 | convolution fusion | flops 536870912 | bytes 9437184 | tf_op jit(solution)/shard_map/pct,qct->cpq/dot_general | solution.py:28
  90.2 1.3 %fusion.19 = f32[8,512,512]{2,1,0:T(8,128)S(1)} fusion(bf16[512,8,128]{2,1,0:T(8,128)(2,1)S(1)} %get-tuple-element.11), kind=kOutput, calls=%fused_computation.34 | convolution fusion | flops 536870912 | bytes 9437184 | tf_op jit(solution)/shard_map/pct,qct->cpq/dot_general | solution.py:28
  91.5 1.3 %fusion.21 = f32[8,512,512]{2,1,0:T(8,128)S(1)} fusion(bf16[512,8,128]{2,1,0:T(8,128)(2,1)S(1)} %get-tuple-element.10), kind=kOutput, calls=%fused_computation.36 | convolution fusion | flops 536870912 | bytes 9437184 | tf_op jit(solution)/shard_map/pct,qct->cpq/dot_general | solution.py:28
  92.7 2.2 %fusion.15 = (bf16[8,1,256,256]{3,2,0,1:T(8,128)(2,1)S(1)}, bf16[8,1,256,256]{3,2,0,1:T(8,128)(2,1)S(1)}) fusion(f32[8,512,512]{2,1,0:T(8,128)S(1)} %fusion.23, f32[8,512,512]{2,1,0:T(8,128)S(1)} %fusion.25), kind=kLoop, calls=%fused_computation.30 | loop fusion | flops 5242880 | bytes 18874368 | tf_op jit(solution)/shard_map/stack | solution.py:61
  94.9 2.2 %fusion.16 = (bf16[8,1,256,256]{3,2,0,1:T(8,128)(2,1)S(1)}, bf16[8,1,256,256]{3,2,0,1:T(8,128)(2,1)S(1)}) fusion(f32[8,512,512]{2,1,0:T(8,128)S(1)} %fusion.19, f32[8,512,512]{2,1,0:T(8,128)S(1)} %fusion.21), kind=kLoop, calls=%fused_computation.31 | loop fusion | flops 5242880 | bytes 18874368 | tf_op jit(solution)/shard_map/stack | solution.py:61
  97.2 0.2 maximum_bitcast_fusion
  97.4 0.2 maximum_bitcast_fusion.1
  97.6 0.4 pad_maximum_fusion
  98.0 2.3 %copy.34 = bf16[2,8,2,256,256]{4,3,2,1,0:T(8,128)(2,1)} copy(bf16[2,8,2,256,256]{4,3,1,2,0:T(8,128)(2,1)S(1)} %pad_maximum_fusion) | data formatting | bytes 8388608 | tf_op jit(solution)/shard_map/stack | solution.py:61
Async XLA Ops:
  61.1 25.8 %collective-permute-start = (bf16[2,256,8,128]{3,2,1,0:T(8,128)(2,1)S(1)}, bf16[2,256,8,128]{3,2,1,0:T(8,128)(2,1)S(1)}, u32[]{:S(2)}, u32[]{:S(2)}) collective-permute-start(bf16[2,256,8,128]{3,2,1,0:T(8,128)(2,1)S(1)} %slice.79), channel_id=1, source_target_pairs={{0,16},{1,17},{2,18},{3,19},{4,20},{5,21},{6,22},{7,23},{8,24},{9,... | collective-permute-start | bytes 3145736 | tf_op jit(solution)/shard_map/ppermute | solution.py:12
where the time goes:
time: 100 us
  blocking collectives  56.5 us (56%)
  waiting for transfers between devices  22 us (22%)
  local copies, waits for them, and re-layouts  6.84 us (7%)
  other arithmetic  6.05 us (6%)
  matrix products  5.05 us (5%)
  starting transfers between devices  3.64 us (4%)
    all_to_all x1, blocking collectives, local(): lax.all_to_all(voltages, ('chan', 'bl'), split_axis=2, concat_axis=1, til...  56.5 us
    ppermute x1, waiting for transfers between devices, passed_along(): return lax.ppermute(block, axis, route)  22 us
    another operation x5, other arithmetic, local(): return jnp.stack([jnp.stack(real_list, 1), jnp.stack(imag_list, 1)], 0)  5.19 us
    dot_general x4, matrix products, products(): jnp.einsum('pct,qct->cpq', stacked, stacked, preferred_element_type=jnp.f...  5.05 us
    ppermute x1, starting transfers between devices, passed_along(): return lax.ppermute(block, axis, route)  3.64 us
    unnamed x1, local copies, waits for them, and re-layouts  2.76 us
    another operation x1, local copies, waits for them, and re-layouts, local(): return jnp.stack([jnp.stack(real_list, 1), jnp.stack(imag_list, 1)], 0)  2.29 us
  transfers between devices with their start and end apart: 1, of which 1 were waited for; matrix products, arithmetic and copies ran while one was open for 0% of the time, Pallas kernels for 0%

commit v1 on v0

--- a/solution.py
+++ b/solution.py
@@ -32,7 +32,10 @@
 
 
 def local(voltages):
-    turned = lax.all_to_all(voltages, ("chan", "bl"), split_axis=2, concat_axis=1, tiled=True)
+    size = lax.axis_size(("chan", "bl"))
+    parts = jnp.stack(jnp.split(voltages, size, axis=2), axis=0)
+    parts = lax.all_to_all(parts, ("chan", "bl"), split_axis=0, concat_axis=0)
+    turned = jnp.concatenate(parts, axis=1)
     signals = turned.shape[1]
     channels = turned.shape[2]
     samples = turned.shape[3]

time: 100 us -> 111 us (1.11)
  local copies, waits for them, and re-layouts: 6.84 us -> 17.2 us
    unnamed x1 -> x15, local copies, waits for them, and re-layouts: 2.76 us -> 13.8 us
    all_to_all x1, local copies, waits for them, and re-layouts: 1.72 us -> 0.14 us  [local(): parts = lax.all_to_all(parts, ('chan', 'bl'), split_axis=0, concat_axis=0)]
where the time goes in v1:
time: 111 us
  blocking collectives  56.5 us (51%)
  waiting for transfers between devices  22.2 us (20%)
  local copies, waits for them, and re-layouts  17.2 us (15%)
  other arithmetic  6.05 us (5%)
  matrix products  5.05 us (5%)
  starting transfers between devices  3.46 us (3%)
    all_to_all x1, blocking collectives, local(): parts = lax.all_to_all(parts, ('chan', 'bl'), split_axis=0, concat_axis=0)  56.5 us
    ppermute x1, waiting for transfers between devices, passed_along(): return lax.ppermute(block, axis, route)  22.2 us
    unnamed x15, local copies, waits for them, and re-layouts  13.8 us
    another operation x5, other arithmetic, local(): return jnp.stack([jnp.stack(real_list, 1), jnp.stack(imag_list, 1)], 0)  5.19 us
    dot_general x4, matrix products, products(): jnp.einsum('pct,qct->cpq', stacked, stacked, preferred_element_type=jnp.f...  5.05 us
    ppermute x1, starting transfers between devices, passed_along(): return lax.ppermute(block, axis, route)  3.46 us
    another operation x1, local copies, waits for them, and re-layouts, local(): return jnp.stack([jnp.stack(real_list, 1), jnp.stack(imag_list, 1)], 0)  2.29 us
  transfers between devices with their start and end apart: 1, of which 1 were waited for; matrix products, arithmetic and copies ran while one was open for 0% of the time, Pallas kernels for 0%

profile of v1, /device:TPU:0, one launch (start us, length us, event | category | flops | bytes accessed | tf_op | source)
XLA Modules:
  0.0 110.6 jit_solution(12216870350781147445)
XLA Ops:
  0.0 0.9 bitcast_dynamic-update-slice_fusion.15
  0.9 0.9 bitcast_dynamic-update-slice_fusion.14
  1.8 0.9 bitcast_dynamic-update-slice_fusion.13
  2.8 0.9 bitcast_dynamic-update-slice_fusion.12
  3.7 0.9 bitcast_dynamic-update-slice_fusion.11
  4.6 0.9 bitcast_dynamic-update-slice_fusion.10
  5.5 0.9 bitcast_dynamic-update-slice_fusion.9
  6.4 0.9 bitcast_dynamic-update-slice_fusion.8
  7.4 0.9 bitcast_dynamic-update-slice_fusion.7
  8.3 0.9 bitcast_dynamic-update-slice_fusion.6
  9.2 0.9 bitcast_dynamic-update-slice_fusion.5
  10.1 0.9 bitcast_dynamic-update-slice_fusion.4
  11.0 0.9 bitcast_dynamic-update-slice_fusion.3
  12.0 0.9 bitcast_dynamic-update-slice_fusion.2
  12.9 0.9 bitcast_dynamic-update-slice_fusion.1
  13.8 0.9 bitcast_dynamic-update-slice_fusion
  14.7 56.5 %all_to_all.5 = bf16[16,2,16,8,256]{4,3,2,1,0:T(8,128)(2,1)S(1)} all-to-all(bf16[16,2,16,8,256]{4,3,2,1,0:T(8,128)(2,1)S(1)} %bitcast_dynamic-update-slice_fusion), channel_id=1, replica_groups=mesh['tm'=2,'chan'=4,'bl'=4] {'chan','bl'}, dimensions={0} | all-to-all | bytes 4194304 | tf_op jit(solution)/shard_map/all_to_all | solution.py:37
  71.2 0.1 copy.12
  71.4 0.1 slice.79
  71.5 3.5 %collective-permute-start = (bf16[2,256,8,128]{3,2,1,0:T(8,128)(2,1)S(1)}, bf16[2,256,8,128]{3,2,1,0:T(8,128)(2,1)S(1)}, u32[]{:S(2)}, u32[]{:S(2)}) collective-permute-start(bf16[2,256,8,128]{3,2,1,0:T(8,128)(2,1)S(1)} %slice.79), channel_id=1, source_target_pairs={{0,16},{1,17},{2,18},{3,19},{4,20},{5,21},{6,22},{7,23},{8,24},{9,... | collective-permute-start | bytes 3145736 | tf_op jit(solution)/shard_map/ppermute | solution.py:12
  74.9 0.1 multiply_sine_fusion
  75.0 22.2 %collective-permute-done = bf16[2,256,8,128]{3,2,1,0:T(8,128)(2,1)S(1)} collective-permute-done((bf16[2,256,8,128]{3,2,1,0:T(8,128)(2,1)S(1)}, bf16[2,256,8,128]{3,2,1,0:T(8,128)(2,1)S(1)}, u32[]{:S(2)}, u32[]{:S(2)}) %collective-permute-start) | collective-permute-done | bytes 1048608 | tf_op jit(solution)/shard_map/ppermute | solution.py:12
  97.2 0.8 fusion
  98.0 1.3 %fusion.23 = f32[8,512,512]{2,1,0:T(8,128)S(1)} fusion(bf16[512,8,128]{2,1,0:T(8,128)(2,1)S(1)} %get-tuple-element.12), kind=kOutput, calls=%fused_computation.38 | convolution fusion | flops 536870912 | bytes 9437184 | tf_op jit(solution)/shard_map/pct,qct->cpq/dot_general | solution.py:28
  99.3 1.3 %fusion.25 = f32[8,512,512]{2,1,0:T(8,128)S(1)} fusion(bf16[512,8,128]{2,1,0:T(8,128)(2,1)S(1)} %get-tuple-element.9), kind=kOutput, calls=%fused_computation.40 | convolution fusion | flops 536870912 | bytes 9437184 | tf_op jit(solution)/shard_map/pct,qct->cpq/dot_general | solution.py:28
  100.6 1.3 %fusion.19 = f32[8,512,512]{2,1,0:T(8,128)S(1)} fusion(bf16[512,8,128]{2,1,0:T(8,128)(2,1)S(1)} %get-tuple-element.11), kind=kOutput, calls=%fused_computation.34 | convolution fusion | flops 536870912 | bytes 9437184 | tf_op jit(solution)/shard_map/pct,qct->cpq/dot_general | solution.py:28
  101.8 1.3 %fusion.21 = f32[8,512,512]{2,1,0:T(8,128)S(1)} fusion(bf16[512,8,128]{2,1,0:T(8,128)(2,1)S(1)} %get-tuple-element.10), kind=kOutput, calls=%fused_computation.36 | convolution fusion | flops 536870912 | bytes 9437184 | tf_op jit(solution)/shard_map/pct,qct->cpq/dot_general | solution.py:28
  103.1 2.2 %fusion.15 = (bf16[8,1,256,256]{3,2,0,1:T(8,128)(2,1)S(1)}, bf16[8,1,256,256]{3,2,0,1:T(8,128)(2,1)S(1)}) fusion(f32[8,512,512]{2,1,0:T(8,128)S(1)} %fusion.23, f32[8,512,512]{2,1,0:T(8,128)S(1)} %fusion.25), kind=kLoop, calls=%fused_computation.30 | loop fusion | flops 5242880 | bytes 18874368 | tf_op jit(solution)/shard_map/stack | solution.py:64
  105.3 2.2 %fusion.16 = (bf16[8,1,256,256]{3,2,0,1:T(8,128)(2,1)S(1)}, bf16[8,1,256,256]{3,2,0,1:T(8,128)(2,1)S(1)}) fusion(f32[8,512,512]{2,1,0:T(8,128)S(1)} %fusion.19, f32[8,512,512]{2,1,0:T(8,128)S(1)} %fusion.21), kind=kLoop, calls=%fused_computation.31 | loop fusion | flops 5242880 | bytes 18874368 | tf_op jit(solution)/shard_map/stack | solution.py:64
  107.5 0.2 maximum_bitcast_fusion
  107.7 0.2 maximum_bitcast_fusion.1
  107.9 0.4 pad_maximum_fusion
  108.3 2.3 %copy.21 = bf16[2,8,2,256,256]{4,3,2,1,0:T(8,128)(2,1)} copy(bf16[2,8,2,256,256]{4,3,1,2,0:T(8,128)(2,1)S(1)} %pad_maximum_fusion) | data formatting | bytes 8388608 | tf_op jit(solution)/shard_map/stack | solution.py:64
Async XLA Ops:
  71.5 25.8 %collective-permute-start = (bf16[2,256,8,128]{3,2,1,0:T(8,128)(2,1)S(1)}, bf16[2,256,8,128]{3,2,1,0:T(8,128)(2,1)S(1)}, u32[]{:S(2)}, u32[]{:S(2)}) collective-permute-start(bf16[2,256,8,128]{3,2,1,0:T(8,128)(2,1)S(1)} %slice.79), channel_id=1, source_target_pairs={{0,16},{1,17},{2,18},{3,19},{4,20},{5,21},{6,22},{7,23},{8,24},{9,... | collective-permute-start | bytes 3145736 | tf_op jit(solution)/shard_map/ppermute | solution.py:12
